TPU v7x, 128 devices: a whole 4x4x4 slice. The times are simulated.
128 devices in a mesh: peer: 32 (over z_hi, x, y), zero: 4 (over z_lo, core).
Axes of the slice: x: 4, y: 4, z: 4 (z_hi: 2, z_lo: 2; z = z_hi * 2 + z_lo), core: 2. Of those that a mesh axis runs over, the one named last changes fastest.
Arguments:
- tokens: bfloat16 [32, 2048, 1024], P('peer', 'zero'), may hold values from -6 to 6
- out_grad: bfloat16 [32, 2048, 1024], P('peer', 'zero'), may hold values from -6 to 6
- step: int32 [1], replicated, may hold values from 0 to 3999
- up_param: float32 [32, 1024, 2048], P('peer', 'zero'), may hold values from -0.2 to 0.2
- down_param: float32 [32, 2048, 1024], P('peer', 'zero'), may hold values from -0.2 to 0.2
- up_first: float32 [32, 1024, 2048], P('peer', 'zero'), may hold values from -27.1529 to 27.1529
- down_first: float32 [32, 2048, 1024], P('peer', 'zero'), may hold values from -27.1529 to 27.1529
- up_second: float32 [32, 1024, 2048], P('peer', 'zero'), may hold values from 0.8192 to 819.2
- down_second: float32 [32, 2048, 1024], P('peer', 'zero'), may hold values from 0.8192 to 819.2
Outputs:
- new_up: float32 [32, 1024, 2048], P('peer', 'zero')
- new_down: float32 [32, 2048, 1024], P('peer', 'zero')
- new_up_first: float32 [32, 1024, 2048], P('peer', 'zero')
- new_down_first: float32 [32, 2048, 1024], P('peer', 'zero')
- new_up_second: float32 [32, 1024, 2048], P('peer', 'zero')
- new_down_second: float32 [32, 2048, 1024], P('peer', 'zero')
All inputs are finite; a program needn't handle non-finite values.
Results may differ from a plain program's by a relative error of at most 0.0065.
Values may be sent and summed in bfloat16 or wider, within the bound.
A program may use at most 128 MiB of HBM per device.

v0:
```python
from functools import partial

import jax
import jax.numpy as jnp
from jax import lax
from jax.sharding import PartitionSpec as P


def for_sending(array):
    return jax.tree.map(lambda a: a.astype(jnp.bfloat16) if a.dtype == jnp.float32 else a, array)


def passed_along(array, axis, by):
    size = lax.axis_size(axis)
    return lax.ppermute(array, axis, [(i, (i + by) % size) for i in range(size)])


def gelu_tanh(values):
    return (
        0.5
        * values
        * (1.0 + jnp.tanh(0.7978845608 * (values + 0.044715 * values * values * values)))
    )


def adam_update(param, first, second, grad, first_fix, second_fix):
    first_new = 0.9 * first + 0.1 * grad
    second_new = 0.999 * second + 0.001 * grad * grad
    local = param - 0.01 * (first_new / first_fix) / (jnp.sqrt(second_new / second_fix) + 1e-08)
    return (local, first_new, second_new)


def across_rows(left, right):
    return lax.dot_general(
        left, right, (((0,), (0,)), ((), ())), preferred_element_type=jnp.float32
    )


def from_partner(pair, by):
    return jax.tree.map(
        lambda part, own: part.astype(own.dtype), passed_along(for_sending(pair), "peer", -by), pair
    )


def body(
    tokens, out_grad, step, up_param, down_param, up_first, down_first, up_second, down_second
):
    grad_rows = out_grad[0]
    widened = tokens[0].astype(jnp.float32)
    center = jnp.mean(widened, axis=1, keepdims=True)
    spread = jnp.mean((widened - center) * (widened - center), axis=1, keepdims=True)
    normed = ((widened - center) * lax.rsqrt(spread + 1e-05)).astype(jnp.bfloat16)
    up_low = up_param[0].astype(jnp.bfloat16)
    down_low = down_param[0].astype(jnp.bfloat16)
    up_whole, down_whole = (
        lax.all_gather(up_low, "zero", axis=0, tiled=True),
        lax.all_gather(down_low, "zero", axis=0, tiled=True),
    )
    pre = jnp.dot(normed, up_whole, preferred_element_type=jnp.float32)
    active, backward = jax.vjp(gelu_tanh, pre)
    act_grad = lax.dot_general(
        grad_rows, down_whole, (((1,), (1,)), ((), ())), preferred_element_type=jnp.float32
    )
    act = active.astype(jnp.bfloat16)
    pre_grad = backward(act_grad)[0].astype(jnp.bfloat16)
    columns = normed
    up_grad = lax.psum_scatter(
        across_rows(columns, pre_grad).astype(jnp.bfloat16), "zero", scatter_dimension=0, tiled=True
    ).astype(jnp.float32)
    columns = act
    down_grad = lax.psum_scatter(
        across_rows(columns, grad_rows).astype(jnp.bfloat16),
        "zero",
        scatter_dimension=0,
        tiled=True,
    ).astype(jnp.float32)
    count = (step[0] + 1).astype(jnp.float32)
    first_fix = 1.0 - jnp.power(jnp.float32(0.9), count)
    second_fix = 1.0 - jnp.power(jnp.float32(0.999), count)
    up_local, up_first_new, up_second_new = adam_update(
        up_param[0], up_first[0], up_second[0], up_grad, first_fix, second_fix
    )
    down_local, down_first_new, down_second_new = adam_update(
        down_param[0], down_first[0], down_second[0], down_grad, first_fix, second_fix
    )
    levels = lax.axis_size("peer").bit_length() - 1
    branches = [partial(from_partner, by=2**level) for level in range(levels)]
    up_other, down_other = lax.switch(step[0] % levels, branches, (up_local, down_local))
    new_up = 0.5 * (up_local + up_other)
    new_down = 0.5 * (down_local + down_other)
    return (
        new_up[None],
        new_down[None],
        up_first_new[None],
        down_first_new[None],
        up_second_new[None],
        down_second_new[None],
    )


def solution(mesh):
    in_specs = (
        P("peer", "zero", None),
        P("peer", "zero", None),
        P(),
        P("peer", "zero", None),
        P("peer", "zero", None),
        P("peer", "zero", None),
        P("peer", "zero", None),
        P("peer", "zero", None),
        P("peer", "zero", None),
    )
    out_specs = (
        P("peer", "zero", None),
        P("peer", "zero", None),
        P("peer", "zero", None),
        P("peer", "zero", None),
        P("peer", "zero", None),
        P("peer", "zero", None),
    )
    return jax.shard_map(body, mesh=mesh, in_specs=in_specs, out_specs=out_specs, check_vma=False)
```

profile of v0, /device:TPU:30, one launch (start us, length us, event | category | flops | bytes accessed | tf_op | source)
XLA Modules:
  0.0 292.8 jit_solution(9134113312605311750)
XLA Ops:
  7.2 2.9 bitcast_convert_fusion.1
  10.2 1.1 bitcast_convert_fusion
  11.4 1.5 convert_reduce_fusion
  12.9 0.4 fusion.9
  13.4 44.8 %all-gather.3.cloned.1.call-done = bf16[1024,2048]{1,0:T(8,128)(2,1)} async-done(((bf16[256,2048]{1,0:T(8,128)(2,1)}), bf16[1024,2048]{1,0:T(8,128)(2,1)}) %all-gather.3.cloned.1.call-update) | async-done | bytes 4194320 | tf_op jit(solution)/shard_map/all_gather | solution.py:56
  58.2 6.6 %fusion.40 = f32[512,2048]{1,0:T(8,128)} fusion(bf16[1024,2048]{1,0:T(8,128)(2,1)} %all-gather.3.cloned.1.call-done, bf16[1,512,1024]{2,1,0:T(8,128)(2,1)S(1)} %copy-done.3, f32[512]{0:T(512)S(1)} %add_rsqrt_fusion, f32[512]{0:T(512)S(1)} %broadcast_multiply_fusion), kind=kOutput, calls=%fused_computation.55 | convolution fusion | flops 2149580800 | bytes 9441280 | tf_op jit(solution)/shard_map/dot_general | solution.py:59
  64.8 43.1 %all-gather.5.cloned.1.call-done = bf16[2048,1024]{1,0:T(8,128)(2,1)} async-done(((bf16[512,1024]{1,0:T(8,128)(2,1)}), bf16[2048,1024]{1,0:T(8,128)(2,1)}) %all-gather.5.cloned.1.call-update) | async-done | bytes 4194320 | tf_op jit(solution)/shard_map/all_gather | solution.py:57
  107.9 11.0 %convolution_convert_fusion.1 = bf16[1024,2048]{1,0:T(8,128)(2,1)} fusion(f32[512,2048]{1,0:T(8,128)} %fusion.40, bf16[2048,1024]{1,0:T(8,128)(2,1)} %all-gather.5.cloned.1.call-done, bf16[1,512,1024]{2,1,0:T(8,128)(2,1)S(1)} %copy-done, bf16[1,512,1024]{2,1,0:T(8,128)(2,1)S(1)} %copy-done.3, f32[512]{0:T(512)S(1)} %add_rsqrt_fusion, ...), kind=kOutput, calls=%fused_computation.12 | convolution fusion | flops 4324327424 | bytes 14684160 | tf_op jit(solution)/shard_map/dot_general | solution.py:34
  119.0 0.2 reduce-scatter.5.cloned.1.call-start
  119.2 7.1 %convolution_convert_fusion = bf16[2048,1024]{1,0:T(8,128)(2,1)} fusion(f32[512,2048]{1,0:T(8,128)} %fusion.40, bf16[1,512,1024]{2,1,0:T(8,128)(2,1)S(1)} %copy-done), kind=kOutput, calls=%fused_computation.11 | convolution fusion | flops 2159017984 | bytes 9437184 | tf_op jit(solution)/shard_map/dot_general | solution.py:34
  127.1 38.9 %reduce-scatter.3.cloned.1.call-done = bf16[256,2048]{1,0:T(8,128)(2,1)} async-done(((bf16[1024,2048]{1,0:T(8,128)(2,1)}), bf16[256,2048]{1,0:T(8,128)(2,1)}) %reduce-scatter.3.cloned.1.call-update) | async-done | bytes 1048592 | tf_op jit(solution)/shard_map/reduce_scatter | solution.py:67
  166.0 6.7 %fusion.23 = (f32[1,256,2048]{2,1,0:T(8,128)}, f32[256,2048]{1,0:T(8,128)S(1)}, f32[1,256,2048]{2,1,0:T(8,128)}) fusion(bf16[256,2048]{1,0:T(8,128)(2,1)} %reduce-scatter.3.cloned.1.call-done, f32[1,256,2048]{2,1,0:T(8,128)} %param.21, f32[]{:T(128)} %bitcast.7, f32[]{:T(128)} %bitcast.5, f32[1,256,2048]{2,1,0:T(8,128)} %param.19, f32[1,256,2048]{2,1,0:T(8,128)} %param.17), kind=kLoop, calls=%fused_computation.41 | loop fusion | flops 7340032 | bytes 13631496 | tf_op jit(solution)/shard_map/broadcast_in_dim | solution.py:96
  172.7 41.9 %reduce-scatter.5.cloned.1.call-done = bf16[512,1024]{1,0:T(8,128)(2,1)} async-done(((bf16[2048,1024]{1,0:T(8,128)(2,1)}), bf16[512,1024]{1,0:T(8,128)(2,1)}) %reduce-scatter.5.cloned.1.call-update) | async-done | bytes 1048592 | tf_op jit(solution)/shard_map/reduce_scatter | solution.py:71
  214.6 7.5 %fusion.22 = (f32[1,512,1024]{2,1,0:T(8,128)}, f32[512,1024]{1,0:T(8,128)}, f32[1,512,1024]{2,1,0:T(8,128)}) fusion(bf16[512,1024]{1,0:T(8,128)(2,1)} %reduce-scatter.5.cloned.1.call-done, f32[1,512,1024]{2,1,0:T(8,128)} %param.22, f32[]{:T(128)} %bitcast.7, f32[]{:T(128)} %bitcast.5, f32[1,512,1024]{2,1,0:T(8,128)} %param.20, f32[1,512,1024]{2,1,0:T(8,128)} %param.18), kind=kLoop, calls=%fused_computation.40 | loop fusion | flops 7340032 | bytes 13631496 | tf_op jit(solution)/shard_map/broadcast_in_dim | solution.py:97
  222.0 56.8 %conditional.4 = (f32[256,2048]{1,0:T(8,128)}, f32[512,1024]{1,0:T(8,128)}) conditional(s32[]{:T(128)} %clamp.3, (f32[256,2048]{1,0:T(8,128)S(1)}, f32[512,1024]{1,0:T(8,128)}) %tuple.60, (f32[256,2048]{1,0:T(8,128)S(1)}, f32[512,1024]{1,0:T(8,128)}) %tuple.60, (f32[256,2048]{1,0:T(8,128)S(1)}, ...), branch_computations={%region_4.5_spmd, %region_5.6_spmd, %region_6.7_spmd, %region_7.8_... | conditional | flops 2097152 | bytes 20971616
  222.0 1.7 convert_element_type.91
  223.8 0.9 collective-permute-start.1
  224.9 0.6 collective-permute-start
  225.5 30.2 %collective-permute-done.1 = bf16[512,1024]{1,0:T(8,128)(2,1)S(1)} collective-permute-done((bf16[512,1024]{1,0:T(8,128)(2,1)S(1)}, bf16[512,1024]{1,0:T(8,128)(2,1)S(1)}, u32[]{:S(2)}, u32[]{:S(2)}) %collective-permute-start.1) | collective-permute-done | bytes 1048608 | tf_op jit(solution)/shard_map/cond/branch_0_fun/ppermute | solution.py:15
  255.6 1.6 convert_element_type.140
  257.2 20.1 %collective-permute-done = bf16[256,2048]{1,0:T(8,128)(2,1)S(1)} collective-permute-done((bf16[256,2048]{1,0:T(8,128)(2,1)S(1)}, bf16[256,2048]{1,0:T(8,128)(2,1)S(1)}, u32[]{:S(2)}, u32[]{:S(2)}) %collective-permute-start) | collective-permute-done | bytes 1048608 | tf_op jit(solution)/shard_map/cond/branch_0_fun/ppermute | solution.py:15
  277.3 1.6 convert_element_type.135
  278.8 4.2 %multiply_bitcast_fusion = f32[1,512,1024]{2,1,0:T(8,128)} fusion(f32[512,1024]{1,0:T(8,128)} %get-tuple-element.59, f32[512,1024]{1,0:T(8,128)} %get-tuple-element.57), kind=kLoop, calls=%fused_computation.32 | loop fusion | flops 1048576 | bytes 6291456 | tf_op jit(solution)/shard_map/broadcast_in_dim | solution.py:93
  283.0 3.3 %multiply_bitcast_fusion.1 = f32[1,256,2048]{2,1,0:T(8,128)} fusion(f32[256,2048]{1,0:T(8,128)S(1)} %get-tuple-element.62, f32[256,2048]{1,0:T(8,128)} %get-tuple-element.56), kind=kLoop, calls=%fused_computation.33 | loop fusion | flops 1048576 | bytes 6291456 | tf_op jit(solution)/shard_map/broadcast_in_dim | solution.py:92
  (18 shorter events, 0.4 us)
Async XLA Ops:
  7.2 100.8 %copy-start = (bf16[1,512,1024]{2,1,0:T(8,128)(2,1)S(1)}, bf16[1,512,1024]{2,1,0:T(8,128)(2,1)}, u32[]{:S(2)}) copy-start(bf16[1,512,1024]{2,1,0:T(8,128)(2,1)} %param.15) | copy-start | bytes 3145732
  7.2 3.0 %copy-start.2 = (f32[1,512,1024]{2,1,0:T(8,128)S(1)}, f32[1,512,1024]{2,1,0:T(8,128)}, u32[]{:S(2)}) copy-start(f32[1,512,1024]{2,1,0:T(8,128)} %param.18) | copy-start | bytes 6291460
  7.2 51.0 %all-gather.3.cloned.1.call-start = ((), (), s32[]{:S(2)}) async-start(), calls=%async_computation.2 | async-start | bytes 5242880 | tf_op jit(solution)/shard_map/all_gather | solution.py:56
  10.1 97.8 %all-gather.5.cloned.1.call-start = ((), (), s32[]{:S(2)}) async-start(), calls=%async_computation.3 | async-start | bytes 5242880 | tf_op jit(solution)/shard_map/all_gather | solution.py:57
  11.3 1.6 copy-start.3
  11.4 154.6 %reduce-scatter.3.cloned.1.call-start = ((), (), s32[]{:S(2)}) async-start(), calls=%async_computation.4 | async-start | bytes 5242880 | tf_op jit(solution)/shard_map/reduce_scatter | solution.py:67
  119.0 95.6 %reduce-scatter.5.cloned.1.call-start = ((), (), s32[]{:S(2)}) async-start(), calls=%async_computation.5 | async-start | bytes 5242880 | tf_op jit(solution)/shard_map/reduce_scatter | solution.py:71
  223.8 31.8 %collective-permute-start.1 = (bf16[512,1024]{1,0:T(8,128)(2,1)S(1)}, bf16[512,1024]{1,0:T(8,128)(2,1)S(1)}, u32[]{:S(2)}, u32[]{:S(2)}) collective-permute-start(bf16[512,1024]{1,0:T(8,128)(2,1)S(1)} %convert_element_type.91), channel_id=1, source_target_pairs={{0,124},{4,0},{8,4},{12,8},{16,12},{20,16},{24,20},{28,24},{32,28}... | collective-permute-start | bytes 3145736 | tf_op jit(solution)/shard_map/cond/branch_0_fun/ppermute | solution.py:15
  224.9 52.4 %collective-permute-start = (bf16[256,2048]{1,0:T(8,128)(2,1)S(1)}, bf16[256,2048]{1,0:T(8,128)(2,1)S(1)}, u32[]{:S(2)}, u32[]{:S(2)}) collective-permute-start(bf16[256,2048]{1,0:T(8,128)(2,1)S(1)} %convert_element_type.89), channel_id=1, source_target_pairs={{0,124},{4,0},{8,4},{12,8},{16,12},{20,16},{24,20},{28,24},{32,28}... | collective-permute-start | bytes 3145736 | tf_op jit(solution)/shard_map/cond/branch_0_fun/ppermute | solution.py:15
  283.0 3.3 %copy-start.1 = (bf16[1,512,1024]{2,1,0:T(8,128)(2,1)S(1)}, bf16[1,512,1024]{2,1,0:T(8,128)(2,1)}, u32[]{:S(2)}) copy-start(bf16[1,512,1024]{2,1,0:T(8,128)(2,1)} %param.15) | copy-start | bytes 3145732
Sparse Core Ops, SparseCore 0:
  10.3 47.9 all-gather.2
  60.4 47.4 all-gather.4
  119.1 46.8 reduce-scatter.2
  168.3 46.2 reduce-scatter.4
where the time goes:
time: 293 us
  waiting for transfers between devices  219 us (75%)
  other arithmetic  32.6 us (11%)
  matrix products  24.8 us (8%)
  between operations  14.6 us (5%)
    ppermute x2, waiting for transfers between devices, passed_along(): lax.ppermute(array, axis, [(i, (i + by) % size) for i in range(size)])  50.2 us
    all_gather x1, waiting for transfers between devices, body(): lax.all_gather(up_low, 'zero', axis=0, tiled=True)  44.8 us
    all_gather x1, waiting for transfers between devices, body(): lax.all_gather(down_low, 'zero', axis=0, tiled=True)  43.1 us
    reduce_scatter x1, waiting for transfers between devices, body(): lax.psum_scatter(across_rows(columns, grad_rows).astype(jnp.bfloat16), 'z...  41.9 us
    reduce_scatter x1, waiting for transfers between devices, body(): lax.psum_scatter(across_rows(columns, pre_grad).astype(jnp.bfloat16), 'ze...  38.9 us
    dot_general x2, matrix products, across_rows(): lax.dot_general(left, right, (((0,), (0,)), ((), ())), preferred_element_...  18.2 us
    broadcast_in_dim x1, other arithmetic, body(): down_second_new[None]  7.47 us
    broadcast_in_dim x1, other arithmetic, body(): up_second_new[None]  6.69 us
  transfers between devices with their start and end apart: 6, of which 6 were waited for; matrix products, arithmetic and copies ran while one was open for 9% of the time, Pallas kernels for 0%

commit v1 on v0

v1 whole, which is shorter than its diff:
```python
from functools import partial

import jax
import jax.numpy as jnp
from jax import lax
from jax.experimental import pallas as pl
from jax.experimental.pallas import tpu as pltpu
from jax.sharding import PartitionSpec as P

MESH = pl.DeviceIdType.MESH
SLICES = 2
CHUNKS = 4
BF16 = jnp.bfloat16
F32 = jnp.float32


def dot(left, right, dims):
    return lax.dot_general(left, right, (dims, ((), ())), preferred_element_type=F32)


def kernel(
    peers,
    distance,
    fix,
    tokens,
    out_grad,
    up_param,
    down_param,
    up_first,
    down_first,
    up_second,
    down_second,
    new_up,
    new_down,
    new_up_first,
    new_down_first,
    new_up_second,
    new_down_second,
    tok,
    grd,
    nrm,
    up_p,
    up_f,
    up_s,
    dn_p,
    dn_f,
    dn_s,
    upw_send,
    upw,
    up_t,
    down_low,
    act,
    slope,
    acc_up,
    acc_down,
    ug_send,
    ug,
    dn_out,
    dn_in,
    up_out,
    up_in,
    load_sem,
    store_sem,
    far_send,
    far_recv,
    relay_send,
    relay_recv,
    near_send,
    near_recv,
    upw_ssem,
    upw_rsem,
    ug_ssem,
    ug_rsem,
    dn_ssem,
    dn_rsem,
    up_ssem,
    up_rsem,
):
    rows, width = tokens.shape
    hid = down_param.shape[0]
    part = up_param.shape[0]
    span = hid // SLICES
    piece = rows // CHUNKS
    block = 2 * piece
    own_blocks = rows // block
    blocks = tok.shape[0]
    near_blocks = 2 * own_blocks

    peer = lax.axis_index("peer")
    me = lax.axis_index("zero")
    mate = me + 1 - 2 * (me % 2)
    cross = (me + 2) % 4
    diagonal = 3 - me
    group = (cross, diagonal, mate)
    onto = (peer + peers - distance) % peers
    source = (peer + distance) % peers

    def local(src, dst, sem):
        return pltpu.make_async_copy(src, dst, sem)

    def remote(src, dst, ssem, rsem, **where):
        return pltpu.make_async_remote_copy(
            src_ref=src, dst_ref=dst, send_sem=ssem, recv_sem=rsem, device_id=where, device_id_type=MESH
        )

    loads = [
        local(up_param, up_p, load_sem.at[0]),
        local(down_param, dn_p, load_sem.at[1]),
        local(down_first, dn_f, load_sem.at[2]),
        local(down_second, dn_s, load_sem.at[3]),
        local(up_first, up_f, load_sem.at[4]),
        local(up_second, up_s, load_sem.at[5]),
    ]
    for b in range(own_blocks):
        at = pl.ds(b * block, block)
        loads.append(local(tokens.at[at], tok.at[b], load_sem.at[6 + 2 * b]))
        loads.append(local(out_grad.at[at], grd.at[b], load_sem.at[7 + 2 * b]))
    loads[0].start()

    barrier = pltpu.get_barrier_semaphore()
    for other in group:
        pl.semaphore_signal(barrier, inc=1, device_id={"zero": other}, device_id_type=MESH)
    for other in (onto, source):
        pl.semaphore_signal(barrier, inc=1, device_id={"peer": other}, device_id_type=MESH)
    for copy in loads[1:]:
        copy.start()

    def far(kind, i):
        src, dst = ((tokens, tok), (out_grad, grd))[kind]
        at = pl.ds(pl.multiple_of(i * piece, piece), piece)
        return remote(
            src.at[at],
            dst.at[near_blocks + i, pl.ds(0, piece)],
            far_send.at[kind, i],
            far_recv.at[kind, i],
            zero=cross,
        )

    def relay(kind, i):
        dst = (tok, grd)[kind]
        return remote(
            dst.at[near_blocks + i, pl.ds(0, piece)],
            dst.at[near_blocks + i, pl.ds(piece, piece)],
            relay_send.at[kind, i],
            relay_recv.at[kind, i],
            zero=mate,
        )

    def near(kind, b):
        src, dst = ((tokens, tok), (out_grad, grd))[kind]
        return remote(
            src.at[pl.ds(b * block, block)],
            dst.at[own_blocks + b],
            near_send.at[kind, b],
            near_recv.at[kind, b],
            zero=mate,
        )

    def weights(s, o):
        return remote(
            upw_send.at[s, group[o]], upw.at[s, me], upw_ssem.at[s, o], upw_rsem.at[s, o], zero=group[o]
        )

    def weights_in(s, o):
        return remote(
            upw_send.at[s, group[o]], upw.at[s, group[o]], upw_ssem.at[s, o], upw_rsem.at[s, o], zero=group[o]
        )

    def grads(s, o):
        return remote(ug_send.at[s, group[o]], ug.at[s, me], ug_ssem.at[s, o], ug_rsem.at[s, o], zero=group[o])

    def grads_in(s, o):
        return remote(
            ug_send.at[s, group[o]], ug.at[s, group[o]], ug_ssem.at[s, o], ug_rsem.at[s, o], zero=group[o]
        )

    def down_away(s, h):
        at = pl.ds(h * (span // 2), span // 2)
        return remote(dn_out.at[s, at], dn_in.at[s, at], dn_ssem.at[s, h], dn_rsem.at[s, h], peer=onto)

    def up_away(s, h):
        at = pl.ds(2 * h, 2)
        return remote(up_out.at[s, at], up_in.at[s, at], up_ssem.at[s, h], up_rsem.at[s, h], peer=onto)

    pl.semaphore_wait(barrier, 5)
    far(0, 0).start()
    for kind in range(2):
        for b in range(own_blocks):
            near(kind, b).start()

    loads[0].wait()
    for s in range(SLICES):

        def lower(j, carry):
            at = pl.ds(pl.multiple_of(j * hid + s * span, span), span)
            upw_send[s, j] = up_p[:, at].astype(BF16)
            return carry

        lax.fori_loop(0, 4, lower, 0)
    for o in range(3):
        weights(0, o).start()
    far(1, 0).start()
    for i in range(1, CHUNKS):
        far(0, i).start()
        far(1, i).start()
    for s in range(1, SLICES):
        for o in range(3):
            weights(s, o).start()

    for s in range(SLICES):
        upw[s, me] = upw_send[s, me]
    loads[1].wait()

    def lower_down(r, carry):
        at = pl.ds(pl.multiple_of(r * (hid // 8), hid // 8), hid // 8)
        down_low[at] = dn_p[at].astype(BF16)
        return carry

    lax.fori_loop(0, 8, lower_down, 0)
    for copy in loads[6:]:
        copy.wait()

    def arrange(s):
        for o in range(3):
            weights_in(s, o).wait_recv()

        def turn(j, carry):
            up_t[:, pl.ds(pl.multiple_of(j * part, part), part)] = upw[s, j].astype(F32).T.astype(BF16)
            return carry

        lax.fori_loop(0, 4, turn, 0)

    def forward(b):
        pre = dot(up_t[...], nrm[b], ((1,), (1,)))
        cube = 0.044715 * pre * pre
        t = jnp.tanh(0.7978845608 * (pre + cube * pre))
        half = 0.5 * (1.0 + t)
        act[...] = (pre * half).astype(BF16)
        slope[...] = half + 0.5 * pre * (1.0 - t * t) * (0.7978845608 * (1.0 + 3.0 * cube))

    def gradients(s, b):
        act_grad = dot(down_low[pl.ds(s * span, span)], grd[b], ((1,), (1,)))
        pre_grad = (act_grad * slope[...]).astype(BF16)
        down = dot(act[...], grd[b], ((1,), (0,)))
        up = dot(pre_grad, nrm[b], ((1,), (0,)))
        acc_down[...] += down
        acc_up[...] += up

    def clear():
        acc_down[...] = jnp.zeros_like(acc_down)
        acc_up[...] = jnp.zeros_like(acc_up)

    def normalise(b):
        step = block // 4

        def some(r, carry):
            at = pl.ds(pl.multiple_of(r * step, step), step)
            wide = tok[b, at].astype(F32)
            center = jnp.mean(wide, axis=1, keepdims=True)
            wide = wide - center
            spread = jnp.mean(wide * wide, axis=1, keepdims=True)
            nrm[b, at] = (wide * lax.rsqrt(spread + 1e-05)).astype(BF16)
            return carry

        lax.fori_loop(0, 4, some, 0)

    def adam(param, first, second, grad):
        first_new = 0.9 * first + 0.1 * grad
        second_new = 0.999 * second + 0.001 * grad * grad
        step = (fix[0] * first_new) / (jnp.sqrt(second_new * fix[1]) + 1e-08)
        return param - step, first_new, second_new

    def down_update(s):
        tall = span // 4

        def some(r, carry):
            here = pl.ds(pl.multiple_of(r * tall, tall), tall)
            at = pl.ds(pl.multiple_of(s * span + r * tall, tall), tall)
            fresh = adam(dn_p[at], dn_f[at], dn_s[at], acc_down[here])
            dn_p[at], dn_f[at], dn_s[at] = fresh
            dn_out[s, here] = fresh[0].astype(BF16)
            return carry

        lax.fori_loop(0, 4, some, 0)

    def up_update(s):
        def some(j, carry):
            at = pl.ds(pl.multiple_of(j * hid + s * span, span), span)
            fresh = adam(up_p[:, at], up_f[:, at], up_s[:, at], ug[s, j].astype(F32))
            up_p[:, at], up_f[:, at], up_s[:, at] = fresh
            up_out[s, j] = fresh[0].astype(BF16)
            return carry

        lax.fori_loop(0, 4, some, 0)

    def share(s):
        def turn(j, carry):
            at = pl.ds(pl.multiple_of(j * part, part), part)
            ug_send[s, j] = acc_up[:, at].T.astype(BF16)
            return carry

        lax.fori_loop(0, 4, turn, 0)

    def down_moments(s):
        at = pl.ds(s * span, span)
        return (
            local(dn_f.at[at], new_down_first.at[at], store_sem.at[4 * s]),
            local(dn_s.at[at], new_down_second.at[at], store_sem.at[4 * s + 1]),
        )

    clear()
    arrange(0)

    def first_pass(b, carry):
        i = jnp.maximum(b - near_blocks, 0)

        @pl.when(jnp.logical_and(b >= own_blocks, b < near_blocks))
        def _():
            remote_near(0, b).wait_recv()

        @pl.when(b >= near_blocks)
        def _():
            far(0, i).wait_recv()
            relay(0, i).start()
            relay(0, i).wait_recv()

        normalise(b)
        forward(b)

        @pl.when(jnp.logical_and(b >= own_blocks, b < near_blocks))
        def _():
            remote_near(1, b).wait_recv()

        @pl.when(b >= near_blocks)
        def _():
            far(1, i).wait_recv()
            relay(1, i).start()
            relay(1, i).wait_recv()

        gradients(0, b)
        return carry

    def remote_near(kind, b):
        src, dst = ((tokens, tok), (out_grad, grd))[kind]
        n = jnp.clip(b - own_blocks, 0, own_blocks - 1)
        return remote(
            src.at[pl.ds(pl.multiple_of(n * block, block), block)],
            dst.at[own_blocks + n],
            near_send.at[kind, n],
            near_recv.at[kind, n],
            zero=mate,
        )

    lax.fori_loop(0, blocks, first_pass, 0)

    for copy in loads[2:6]:
        copy.wait()
    down_update(0)
    share(0)
    for h in range(2):
        down_away(0, h).start()
    for copy in down_moments(0):
        copy.start()
    ug[0, me] = ug_send[0, me]
    for o in range(3):
        grads(0, o).start()

    clear()
    arrange(1)

    def second_pass(b, carry):
        @pl.when(b == blocks // 2)
        def _():
            for o in range(3):
                grads_in(0, o).wait_recv()
            up_update(0)
            for h in range(2):
                up_away(0, h).start()

        forward(b)
        gradients(1, b)
        return carry

    lax.fori_loop(0, blocks, second_pass, 0)
    share(1)
    down_update(1)
    for o in range(3):
        grads(1, o).start()
    ug[1, me] = ug_send[1, me]
    for h in range(2):
        down_away(1, h).start()
    for copy in down_moments(1):
        copy.start()

    def down_mean(s, h):
        here = pl.ds(h * (span // 2), span // 2)
        at = pl.ds(s * span + h * (span // 2), span // 2)
        down_away(s, h).wait_recv()
        dn_p[at] = 0.5 * (dn_p[at] + dn_in[s, here].astype(F32))
        local(dn_p.at[at], new_down.at[at], store_sem.at[8 + 2 * s + h]).start()

    def up_mean_copy(s, j):
        at = pl.ds(j * hid + s * span, span)
        return local(up_p.at[:, at], new_up.at[:, at], store_sem.at[12 + 4 * s + j])

    def up_mean(s, h):
        up_away(s, h).wait_recv()
        for j in (2 * h, 2 * h + 1):
            at = pl.ds(j * hid + s * span, span)
            up_p[:, at] = 0.5 * (up_p[:, at] + up_in[s, j].astype(F32))
            up_mean_copy(s, j).start()

    for h in range(2):
        down_mean(0, h)
    for o in range(3):
        grads_in(1, o).wait_recv()
    up_update(1)
    for h in range(2):
        up_away(1, h).start()
    up_moments = (
        local(up_f, new_up_first, store_sem.at[2]),
        local(up_s, new_up_second, store_sem.at[3]),
    )
    for copy in up_moments:
        copy.start()
    for h in range(2):
        up_mean(0, h)
    for h in range(2):
        down_mean(1, h)
    for h in range(2):
        up_mean(1, h)

    for kind in range(2):
        for i in range(CHUNKS):
            far(kind, i).wait_send()
            relay(kind, i).wait_send()
        for b in range(own_blocks):
            near(kind, b).wait_send()
    for s in range(SLICES):
        for o in range(3):
            weights(s, o).wait_send()
            grads(s, o).wait_send()
        for h in range(2):
            down_away(s, h).wait_send()
            up_away(s, h).wait_send()
        for copy in down_moments(s):
            copy.wait()
        for h in range(2):
            at = pl.ds(s * span + h * (span // 2), span // 2)
            local(dn_p.at[at], new_down.at[at], store_sem.at[8 + 2 * s + h]).wait()
        for j in range(4):
            up_mean_copy(s, j).wait()
    for copy in up_moments:
        copy.wait()


def fused(level, peers, fix, *arrays):
    tokens, out_grad, up_param, down_param = arrays[:4]
    rows, width = tokens.shape
    hid = down_param.shape[0]
    part, full = up_param.shape
    span = hid // SLICES
    piece = rows // CHUNKS
    block = 2 * piece
    blocks = 4 * rows // block
    own_blocks = rows // block
    dma = pltpu.SemaphoreType.DMA
    vmem = pltpu.VMEM
    shapes = [
        jax.ShapeDtypeStruct(up_param.shape, F32),
        jax.ShapeDtypeStruct(down_param.shape, F32),
    ] * 3
    return pl.pallas_call(
        partial(kernel, peers, 2**level),
        out_shape=shapes,
        in_specs=[pl.BlockSpec(memory_space=pltpu.SMEM)] + [pl.BlockSpec(memory_space=pl.ANY)] * 8,
        out_specs=[pl.BlockSpec(memory_space=pl.ANY)] * 6,
        scratch_shapes=[
            vmem((blocks, block, width), BF16),
            vmem((blocks, block, width), BF16),
            vmem((blocks, block, width), BF16),
            vmem((part, full), F32),
            vmem((part, full), F32),
            vmem((part, full), F32),
            vmem((hid, width), F32),
            vmem((hid, width), F32),
            vmem((hid, width), F32),
            vmem((SLICES, 4, part, span), BF16),
            vmem((SLICES, 4, part, span), BF16),
            vmem((span, width), BF16),
            vmem((hid, width), BF16),
            vmem((span, block), BF16),
            vmem((span, block), F32),
            vmem((span, width), F32),
            vmem((span, width), F32),
            vmem((SLICES, 4, part, span), BF16),
            vmem((SLICES, 4, part, span), BF16),
            vmem((SLICES, span, width), BF16),
            vmem((SLICES, span, width), BF16),
            vmem((SLICES, 4, part, span), BF16),
            vmem((SLICES, 4, part, span), BF16),
            dma((6 + 2 * own_blocks,)),
            dma((12 + 4 * SLICES,)),
            dma((2, CHUNKS)),
            dma((2, CHUNKS)),
            dma((2, CHUNKS)),
            dma((2, CHUNKS)),
            dma((2, own_blocks)),
            dma((2, own_blocks)),
            dma((SLICES, 3)),
            dma((SLICES, 3)),
            dma((SLICES, 3)),
            dma((SLICES, 3)),
            dma((SLICES, 2)),
            dma((SLICES, 2)),
            dma((SLICES, 2)),
            dma((SLICES, 2)),
        ],
        compiler_params=pltpu.CompilerParams(
            collective_id=level, has_side_effects=True, vmem_limit_bytes=60 * 1024 * 1024
        ),
        name="adam_step",
    )(fix, *arrays)


def body(
    tokens, out_grad, step, up_param, down_param, up_first, down_first, up_second, down_second
):
    peers = lax.axis_size("peer")
    count = (step[0] + 1).astype(F32)
    first_fix = 1.0 - jnp.power(F32(0.9), count)
    second_fix = 1.0 - jnp.power(F32(0.999), count)
    fix = jnp.stack([0.01 / first_fix, 1.0 / second_fix])
    levels = peers.bit_length() - 1
    arrays = [
        a[0]
        for a in (
            tokens, out_grad, up_param, down_param, up_first, down_first, up_second, down_second
        )
    ]
    branches = [partial(fused, level, peers) for level in range(levels)]
    outs = lax.switch(step[0] % levels, branches, fix, *arrays)
    return tuple(o[None] for o in outs)


def solution(mesh):
    sharded = P("peer", "zero", None)
    return jax.shard_map(
        body,
        mesh=mesh,
        in_specs=(sharded, sharded, P()) + (sharded,) * 6,
        out_specs=(sharded,) * 6,
        check_vma=False,
    )
```

time: 293 us -> 165 us (0.56)
  waiting for transfers between devices: 219 us -> 0 us
  Pallas kernels: 0 us -> 148 us
  other arithmetic: 32.6 us -> 0.08 us
  matrix products: 24.8 us -> 0 us
  between operations: 14.6 us -> 1.48 us
  local copies, waits for them, and re-layouts: 0.03 us -> 13 us
    pallas_call x0 -> x1, Pallas kernels: none -> 148 us  [fused(): pl.pallas_call(partial(kernel, peers, 2 ** level), out_shape=shapes, in_s...]
    all_gather x2 -> x0, waiting for transfers between devices: 88 us -> none  [the longest x1 44.8 us: body(): lax.all_gather(up_low, 'zero', axis=0, tiled=True)]
    reduce_scatter x2 -> x0, waiting for transfers between devices: 80.8 us -> none  [the longest x1 41.9 us: body(): lax.psum_scatter(across_rows(columns, grad_rows).astype(jnp.bfloat16), 'z...]
    ppermute x2 -> x0, waiting for transfers between devices: 50.2 us -> none  [passed_along(): lax.ppermute(array, axis, [(i, (i + by) % size) for i in range(size)])]
    dot_general x3 -> x0, matrix products: 24.8 us -> none  [the longest x2 18.2 us: across_rows(): lax.dot_general(left, right, (((0,), (0,)), ((), ())), preferred_element_...]
    broadcast_in_dim x4 -> x0, other arithmetic: 21.6 us -> none  [the longest x1 7.47 us: body(): down_second_new[None]]
    unnamed x8 -> x16, local copies, waits for them, and re-layouts: 0.03 us -> 13 us
    convert_element_type x6 -> x0, other arithmetic: 9.03 us -> none  [the longest x2 3.15 us: from_partner(): part.astype(own.dtype)]
  transfers between devices with their start and end apart: 6 -> 0, of which waited for: 6 -> 0; matrix products, arithmetic and copies ran while one was open for 9% -> 0% of each run, Pallas kernels for 0% -> 0%
where the time goes in v1:
time: 165 us; the launch traced here: 163 us
  Pallas kernels  148 us (90%)
  local copies, waits for them, and re-layouts  13 us (8%)
    pallas_call x1, Pallas kernels, fused(): pl.pallas_call(partial(kernel, peers, 2 ** level), out_shape=shapes, in_s...  148 us
    unnamed x16, local copies, waits for them, and re-layouts  13 us

profile of v1, /device:TPU:30, one launch (start us, length us, event | category | flops | bytes accessed | tf_op | source)
XLA Modules:
  0.0 163.0 jit_solution(2997495374347119416)
XLA Ops:
  1.5 0.1 pad_maximum_fusion
  1.5 148.4 %conditional.1 = ((f32[256,2048]{1,0:T(8,128)S(1)}, f32[512,1024]{1,0:T(8,128)}, f32[256,2048]{1,0:T(8,128)}, f32[512,1024]{1,0:T(8,128)}, f32[256,2048]{1,0:T(8,128)}, /*index=5*/f32[512,1024]{1,0:T(8,128)})) conditional(s32[]{:T(128)} %clamp.3, (bf16[1,512,1024]{2,1,0:T(8,128)(2,1)}, ...), branch_computations={%region_0.1_spmd, %region_1.2_spmd, %region_2.3_spmd, %region_3.4_... | conditional | bytes 8 | solution.py:542
  1.7 148.0 %adam_step.7 = (f32[256,2048]{1,0:T(8,128)S(1)}, f32[512,1024]{1,0:T(8,128)}, f32[256,2048]{1,0:T(8,128)}, f32[512,1024]{1,0:T(8,128)}, f32[256,2048]{1,0:T(8,128)}, /*index=5*/f32[512,1024]{1,0:T(8,128)}) custom-call(f32[2]{0:T(128)S(1)} %get-tuple-element.196.fix, bf16[512,1024]{1,0:T(8,128)(2,1)} %bitcast.79, bf16[512,1024]{1,0:T(8,128)(2,1)} %bitcast.84, ...), custom_call_target="tpu_custom_call" | custom-call | tf_op jit(solution)/shard_map/cond/branch_2_fun/adam_step/pallas_call | solution.py:473
  149.9 0.0 copy-start
  149.9 1.3 copy.52
  151.2 1.0 copy-done
  152.3 0.0 copy-start.1
  152.3 1.3 copy.53
  153.6 1.0 copy-done.1
  154.6 0.0 copy-start.2
  154.6 1.3 copy.54
  155.9 1.0 copy-done.2
  157.0 0.0 copy-start.3
  157.0 1.3 copy.55
  158.3 1.0 copy-done.3
  159.3 0.0 copy-start.4
  159.3 1.3 copy.56
  160.6 1.0 copy-done.4
  161.7 1.3 copy.57
Async XLA Ops:
  149.9 2.3 %copy-start = (f32[512,1024]{1,0:T(8,128)S(1)}, f32[512,1024]{1,0:T(8,128)}, u32[]{:S(2)}) copy-start(f32[512,1024]{1,0:T(8,128)} %get-tuple-element.252) | copy-start | bytes 6291460
  152.3 2.3 %copy-start.1 = (f32[256,2048]{1,0:T(8,128)S(1)}, f32[256,2048]{1,0:T(8,128)}, u32[]{:S(2)}) copy-start(f32[256,2048]{1,0:T(8,128)} %get-tuple-element.251) | copy-start | bytes 6291460
  154.6 2.3 %copy-start.2 = (f32[512,1024]{1,0:T(8,128)S(1)}, f32[512,1024]{1,0:T(8,128)}, u32[]{:S(2)}) copy-start(f32[512,1024]{1,0:T(8,128)} %get-tuple-element.250) | copy-start | bytes 6291460
  157.0 2.3 %copy-start.3 = (f32[256,2048]{1,0:T(8,128)S(1)}, f32[256,2048]{1,0:T(8,128)}, u32[]{:S(2)}) copy-start(f32[256,2048]{1,0:T(8,128)} %get-tuple-element.249) | copy-start | bytes 6291460
  159.3 2.3 %copy-start.4 = (f32[512,1024]{1,0:T(8,128)S(1)}, f32[512,1024]{1,0:T(8,128)}, u32[]{:S(2)}) copy-start(f32[512,1024]{1,0:T(8,128)} %get-tuple-element.248) | copy-start | bytes 6291460

commit v2 on v1

--- a/solution.py
+++ b/solution.py
@@ -30,21 +30,15 @@
     down_first,
     up_second,
     down_second,
-    new_up,
-    new_down,
-    new_up_first,
-    new_down_first,
-    new_up_second,
-    new_down_second,
+    up_p,
+    dn_p,
+    up_f,
+    dn_f,
+    up_s,
+    dn_s,
     tok,
     grd,
     nrm,
-    up_p,
-    up_f,
-    up_s,
-    dn_p,
-    dn_f,
-    dn_s,
     upw_send,
     upw,
     up_t,
@@ -59,8 +53,9 @@
     dn_in,
     up_out,
     up_in,
+    dn_z,
+    up_z,
     load_sem,
-    store_sem,
     far_send,
     far_recv,
     relay_send,
@@ -75,6 +70,8 @@
     dn_rsem,
     up_ssem,
     up_rsem,
+    z_ssem,
+    z_rsem,
 ):
     rows, width = tokens.shape
     hid = down_param.shape[0]
@@ -92,8 +89,18 @@
     cross = (me + 2) % 4
     diagonal = 3 - me
     group = (cross, diagonal, mate)
-    onto = (peer + peers - distance) % peers
-    source = (peer + distance) % peers
+    half = peers // 2
+    twin = (peer + half) % peers
+    if distance < half:
+        upper = peer // half
+        place = peer % half
+        sends_on = place < distance
+        gets_on = place + distance >= half
+        onto = upper * half + (place + half - distance) % half
+        source = upper * half + (place + distance) % half
+    else:
+        sends_on = gets_on = None
+        onto = source = twin
 
     def local(src, dst, sem):
         return pltpu.make_async_copy(src, dst, sem)
@@ -120,7 +127,8 @@
     barrier = pltpu.get_barrier_semaphore()
     for other in group:
         pl.semaphore_signal(barrier, inc=1, device_id={"zero": other}, device_id_type=MESH)
-    for other in (onto, source):
+    others = (onto, source) if sends_on is None else (onto, source, twin)
+    for other in others:
         pl.semaphore_signal(barrier, inc=1, device_id={"peer": other}, device_id_type=MESH)
     for copy in loads[1:]:
         copy.start()
@@ -174,15 +182,38 @@
             ug_send.at[s, group[o]], ug.at[s, group[o]], ug_ssem.at[s, o], ug_rsem.at[s, o], zero=group[o]
         )
 
-    def down_away(s, h):
-        at = pl.ds(h * (span // 2), span // 2)
-        return remote(dn_out.at[s, at], dn_in.at[s, at], dn_ssem.at[s, h], dn_rsem.at[s, h], peer=onto)
-
-    def up_away(s, h):
-        at = pl.ds(2 * h, 2)
-        return remote(up_out.at[s, at], up_in.at[s, at], up_ssem.at[s, h], up_rsem.at[s, h], peer=onto)
-
-    pl.semaphore_wait(barrier, 5)
+    def cut(s, k):
+        if k < 2:
+            at = pl.ds(k * (span // 2), span // 2)
+            return [ref.at[s, at] for ref in (dn_out, dn_in, dn_z)]
+        at = pl.ds(2 * (k - 2), 2)
+        return [ref.at[s, at] for ref in (up_out, up_in, up_z)]
+
+    def away(s, k):
+        out, into, _ = cut(s, k)
+        sem = (dn_ssem, dn_rsem) if k < 2 else (up_ssem, up_rsem)
+        return remote(out, into, sem[0].at[s, k % 2], sem[1].at[s, k % 2], peer=onto)
+
+    def away_later(s, k):
+        _, into, along = cut(s, k)
+        sem = (dn_ssem, dn_rsem) if k < 2 else (up_ssem, up_rsem)
+        return remote(along, into, sem[0].at[s, k % 2], sem[1].at[s, k % 2], peer=onto)
+
+    def along_z(s, k):
+        out, into, along = cut(s, k)
+        return remote(out if s else into, along, z_ssem.at[s, k], z_rsem.at[s, k], peer=twin)
+
+    def when(flag, run):
+        if flag is not None:
+            pl.when(flag)(run)
+
+    def when_not(flag, run):
+        if flag is None:
+            run()
+        else:
+            pl.when(jnp.logical_not(flag))(run)
+
+    pl.semaphore_wait(barrier, len(group) + len(others))
     far(0, 0).start()
     for kind in range(2):
         for b in range(own_blocks):
@@ -301,13 +332,6 @@
 
         lax.fori_loop(0, 4, turn, 0)
 
-    def down_moments(s):
-        at = pl.ds(s * span, span)
-        return (
-            local(dn_f.at[at], new_down_first.at[at], store_sem.at[4 * s]),
-            local(dn_s.at[at], new_down_second.at[at], store_sem.at[4 * s + 1]),
-        )
-
     clear()
     arrange(0)
 
@@ -357,10 +381,8 @@
         copy.wait()
     down_update(0)
     share(0)
-    for h in range(2):
-        down_away(0, h).start()
-    for copy in down_moments(0):
-        copy.start()
+    for k in range(2):
+        away(0, k).start()
     ug[0, me] = ug_send[0, me]
     for o in range(3):
         grads(0, o).start()
@@ -374,8 +396,8 @@
             for o in range(3):
                 grads_in(0, o).wait_recv()
             up_update(0)
-            for h in range(2):
-                up_away(0, h).start()
+            for k in range(2, 4):
+                away(0, k).start()
 
         forward(b)
         gradients(1, b)
@@ -387,48 +409,71 @@
     for o in range(3):
         grads(1, o).start()
     ug[1, me] = ug_send[1, me]
-    for h in range(2):
-        down_away(1, h).start()
-    for copy in down_moments(1):
-        copy.start()
-
-    def down_mean(s, h):
-        here = pl.ds(h * (span // 2), span // 2)
-        at = pl.ds(s * span + h * (span // 2), span // 2)
-        down_away(s, h).wait_recv()
-        dn_p[at] = 0.5 * (dn_p[at] + dn_in[s, here].astype(F32))
-        local(dn_p.at[at], new_down.at[at], store_sem.at[8 + 2 * s + h]).start()
-
-    def up_mean_copy(s, j):
-        at = pl.ds(j * hid + s * span, span)
-        return local(up_p.at[:, at], new_up.at[:, at], store_sem.at[12 + 4 * s + j])
-
-    def up_mean(s, h):
-        up_away(s, h).wait_recv()
-        for j in (2 * h, 2 * h + 1):
-            at = pl.ds(j * hid + s * span, span)
-            up_p[:, at] = 0.5 * (up_p[:, at] + up_in[s, j].astype(F32))
-            up_mean_copy(s, j).start()
-
-    for h in range(2):
-        down_mean(0, h)
+
+    def start_down():
+        for k in range(2):
+            away(1, k).start()
+
+    when_not(sends_on, start_down)
+
     for o in range(3):
         grads_in(1, o).wait_recv()
     up_update(1)
-    for h in range(2):
-        up_away(1, h).start()
-    up_moments = (
-        local(up_f, new_up_first, store_sem.at[2]),
-        local(up_s, new_up_second, store_sem.at[3]),
-    )
-    for copy in up_moments:
-        copy.start()
-    for h in range(2):
-        up_mean(0, h)
-    for h in range(2):
-        down_mean(1, h)
-    for h in range(2):
-        up_mean(1, h)
+
+    def start_up():
+        for k in range(2, 4):
+            away(1, k).start()
+
+    when_not(sends_on, start_up)
+    for o in range(3):
+        grads(1, o).wait_send()
+
+    def pass_on():
+        for k in range(4):
+            away(0, k).wait_recv()
+            along_z(0, k).start()
+
+    when(gets_on, pass_on)
+
+    def start_along():
+        for k in range(4):
+            along_z(1, k).start()
+
+    when(sends_on, start_along)
+
+    def go_on():
+        for k in range(4):
+            along_z(1, k).wait_recv()
+            away_later(1, k).start()
+
+    when(sends_on, go_on)
+
+    def mean(s, k, down, up):
+        if k < 2:
+            tall = span // 2
+            here = pl.ds(k * tall, tall)
+            at = pl.ds(s * span + k * tall, tall)
+            dn_p[at] = 0.5 * (dn_p[at] + down[s, here].astype(F32))
+        else:
+            for j in (2 * k - 4, 2 * k - 3):
+                at = pl.ds(j * hid + s * span, span)
+                up_p[:, at] = 0.5 * (up_p[:, at] + up[s, j].astype(F32))
+
+    def means_near():
+        for k in range(4):
+            away(0, k).wait_recv()
+            mean(0, k, dn_in, up_in)
+
+    def means_along():
+        for k in range(4):
+            along_z(0, k).wait_recv()
+            mean(0, k, dn_z, up_z)
+
+    when_not(gets_on, means_near)
+    when(gets_on, means_along)
+    for k in range(4):
+        away(1, k).wait_recv()
+        mean(1, k, dn_in, up_in)
 
     for kind in range(2):
         for i in range(CHUNKS):
@@ -439,19 +484,39 @@
     for s in range(SLICES):
         for o in range(3):
             weights(s, o).wait_send()
-            grads(s, o).wait_send()
-        for h in range(2):
-            down_away(s, h).wait_send()
-            up_away(s, h).wait_send()
-        for copy in down_moments(s):
-            copy.wait()
-        for h in range(2):
-            at = pl.ds(s * span + h * (span // 2), span // 2)
-            local(dn_p.at[at], new_down.at[at], store_sem.at[8 + 2 * s + h]).wait()
-        for j in range(4):
-            up_mean_copy(s, j).wait()
-    for copy in up_moments:
+    for o in range(3):
+        grads(0, o).wait_send()
+    for s in range(SLICES):
+        for k in range(4):
+            away(s, k).wait_send()
+
+    def sent_along(s):
+        for k in range(4):
+            along_z(s, k).wait_send()
+
+    when(gets_on, partial(sent_along, 0))
+    when(sends_on, partial(sent_along, 1))
+
+
+def flush_kernel(*refs):
+    held, out, sem = refs[:6], refs[6:12], refs[12]
+    copies = [pltpu.make_async_copy(held[i], out[i], sem.at[i]) for i in range(6)]
+    for copy in copies:
+        copy.start()
+    for copy in copies:
         copy.wait()
+
+
+def flush(*arrays):
+    return pl.pallas_call(
+        flush_kernel,
+        out_shape=[jax.ShapeDtypeStruct(a.shape, a.dtype) for a in arrays],
+        in_specs=[pl.BlockSpec(memory_space=pl.ANY)] * 6,
+        out_specs=[pl.BlockSpec(memory_space=pl.ANY)] * 6,
+        scratch_shapes=[pltpu.SemaphoreType.DMA((6,))],
+        compiler_params=pltpu.CompilerParams(vmem_limit_bytes=4 * 1024 * 1024),
+        name="flush",
+    )(*arrays)
 
 
 def fused(level, peers, fix, *arrays):
@@ -467,24 +532,18 @@
     dma = pltpu.SemaphoreType.DMA
     vmem = pltpu.VMEM
     shapes = [
-        jax.ShapeDtypeStruct(up_param.shape, F32),
-        jax.ShapeDtypeStruct(down_param.shape, F32),
+        pltpu.VMEM(up_param.shape, F32),
+        pltpu.VMEM(down_param.shape, F32),
     ] * 3
     return pl.pallas_call(
         partial(kernel, peers, 2**level),
         out_shape=shapes,
         in_specs=[pl.BlockSpec(memory_space=pltpu.SMEM)] + [pl.BlockSpec(memory_space=pl.ANY)] * 8,
-        out_specs=[pl.BlockSpec(memory_space=pl.ANY)] * 6,
+        out_specs=[pl.BlockSpec(memory_space=pltpu.VMEM)] * 6,
         scratch_shapes=[
             vmem((blocks, block, width), BF16),
             vmem((blocks, block, width), BF16),
             vmem((blocks, block, width), BF16),
-            vmem((part, full), F32),
-            vmem((part, full), F32),
-            vmem((part, full), F32),
-            vmem((hid, width), F32),
-            vmem((hid, width), F32),
-            vmem((hid, width), F32),
             vmem((SLICES, 4, part, span), BF16),
             vmem((SLICES, 4, part, span), BF16),
             vmem((span, width), BF16),
@@ -499,8 +558,9 @@
             vmem((SLICES, span, width), BF16),
             vmem((SLICES, 4, part, span), BF16),
             vmem((SLICES, 4, part, span), BF16),
+            vmem((SLICES, span, width), BF16),
+            vmem((SLICES, 4, part, span), BF16),
             dma((6 + 2 * own_blocks,)),
-            dma((12 + 4 * SLICES,)),
             dma((2, CHUNKS)),
             dma((2, CHUNKS)),
             dma((2, CHUNKS)),
@@ -515,12 +575,18 @@
             dma((SLICES, 2)),
             dma((SLICES, 2)),
             dma((SLICES, 2)),
+            dma((SLICES, 4)),
+            dma((SLICES, 4)),
         ],
         compiler_params=pltpu.CompilerParams(
-            collective_id=level, has_side_effects=True, vmem_limit_bytes=60 * 1024 * 1024
+            collective_id=level, has_side_effects=True, vmem_limit_bytes=46 * 1024 * 1024
         ),
         name="adam_step",
     )(fix, *arrays)
+
+
+def step_at(level, peers, fix, *arrays):
+    return flush(*fused(level, peers, fix, *arrays))
 
 
 def body(
@@ -538,7 +604,7 @@
             tokens, out_grad, up_param, down_param, up_first, down_first, up_second, down_second
         )
     ]
-    branches = [partial(fused, level, peers) for level in range(levels)]
+    branches = [partial(step_at, level, peers) for level in range(levels)]
     outs = lax.switch(step[0] % levels, branches, fix, *arrays)
     return tuple(o[None] for o in outs)
 

time: 165 us -> 124 us (0.75); the launches traced: 163 us -> 124 us
  Pallas kernels: 148 us -> 122 us
  local copies, waits for them, and re-layouts: 13 us -> 0 us
    pallas_call x1, Pallas kernels: 148 us -> 117 us  [fused(): pl.pallas_call(partial(kernel, peers, 2 ** level), out_shape=shapes, in_s...]
    unnamed x16 -> x0, local copies, waits for them, and re-layouts: 13 us -> none
    pallas_call x0 -> x1, Pallas kernels: none -> 4.65 us  [flush(): pl.pallas_call(flush_kernel, out_shape=[jax.ShapeDtypeStruct(a.shape, a.d...]
where the time goes in v2:
time: 124 us
  Pallas kernels  122 us (98%)
  between operations  1.64 us (1%)
    pallas_call x1, Pallas kernels, fused(): pl.pallas_call(partial(kernel, peers, 2 ** level), out_shape=shapes, in_s...  117 us
    pallas_call x1, Pallas kernels, flush(): pl.pallas_call(flush_kernel, out_shape=[jax.ShapeDtypeStruct(a.shape, a.d...  4.65 us

profile of v2, /device:TPU:30, one launch (start us, length us, event | category | flops | bytes accessed | tf_op | source)
XLA Modules:
  0.0 123.9 jit_solution(16979762185651990532)
XLA Ops:
  1.5 0.1 pad_maximum_fusion
  1.5 122.1 %conditional.1 = ((f32[256,2048]{1,0:T(8,128)}, f32[512,1024]{1,0:T(8,128)}, f32[256,2048]{1,0:T(8,128)}, f32[512,1024]{1,0:T(8,128)}, f32[256,2048]{1,0:T(8,128)}, /*index=5*/f32[512,1024]{1,0:T(8,128)})) conditional(s32[]{:T(128)} %clamp.3, (bf16[1,512,1024]{2,1,0:T(8,128)(2,1)}, bf16[1,512,1024]{2,1,0:T(8,128)(2,1)}, ...), branch_computations={%region_0.1_spmd.clone, %region_1.2_spmd.clone, %region_2.3_spmd.c... | conditional | bytes 8 | solution.py:608
  1.5 117.3 %adam_step.5 = (f32[256,2048]{1,0:T(8,128)S(1)}, f32[512,1024]{1,0:T(8,128)S(1)}, f32[256,2048]{1,0:T(8,128)S(1)}, f32[512,1024]{1,0:T(8,128)S(1)}, f32[256,2048]{1,0:T(8,128)S(1)}, /*index=5*/f32[512,1024]{1,0:T(8,128)S(1)}) custom-call(f32[2]{0:T(128)S(1)} %get-tuple-element.285.fix, bf16[512,1024]{1,0:T(8,128)(2,1)} %bitcast.77, ...), custom_call_target="tpu_custom_call" | custom-call | tf_op jit(solution)/shard_map/cond/branch_0_fun/adam_step/pallas_call | solution.py:538
  118.8 4.6 %flush.5 = (f32[256,2048]{1,0:T(8,128)}, f32[512,1024]{1,0:T(8,128)}, f32[256,2048]{1,0:T(8,128)}, f32[512,1024]{1,0:T(8,128)}, f32[256,2048]{1,0:T(8,128)}, /*index=5*/f32[512,1024]{1,0:T(8,128)}) custom-call(f32[256,2048]{1,0:T(8,128)S(1)} %get-tuple-element.294.refs_0_, f32[512,1024]{1,0:T(8,128)S(1)} %get-tuple-element.295.refs_1_, ...), custom_call_target="tpu_custom_call" | custom-call | tf_op jit(solution)/shard_map/cond/branch_0_fun/flush/pallas_call | solution.py:511
